TPU v7x, 128 devices: a whole 4x4x4 slice. The times are simulated.
128 devices in a mesh: row: 8 (over x_lo, z), col: 16 (over y, x_hi, core).
Axes of the slice: x: 4 (x_hi: 2, x_lo: 2; x = x_hi * 2 + x_lo), y: 4, z: 4, core: 2. Of those that a mesh axis runs over, the one named last changes fastest.
Arguments:
- lensed_picture_vectors: bfloat16 [24576, 512], P(('row', 'col')), may hold values from -6 to 6
- theta_feature_vectors: bfloat16 [24576, 512], P(('row', 'col')), may hold values from -6 to 6
- prior_domain_label: int32 [24576], P(('row', 'col')), may hold values from 0 to 63, as said below
- matched_theta_index: int32 [24576], P(('row', 'col')), may hold values from 0 to 24575, each once
- affinity_gain: float32 [1], replicated, may hold values from 5 to 15
- affinity_shift: float32 [1], replicated, may hold values from -4 to -1
Outputs:
- loss: float32 [1], replicated
- grad_data: float32 [24576, 512], P(('row', 'col'))
- grad_param: float32 [24576, 512], P(('row', 'col'))
Inputs may be any that keep to these rules, and one draw needn't show every extreme that they name: `matched_theta_index`: a permutation of the pair indices. `prior_domain_label`: region 0 is shared by a share of the pairs that differs between blocks of 192 pairs.
All inputs are finite; a program needn't handle non-finite values.
Results may differ from a plain program's by a relative error of at most 0.00086.
Values may be sent and summed in bfloat16 or wider, within the bound.
A program may use at most 64 MiB of HBM per device.

v0:
```python
import functools

import jax
import jax.numpy as jnp
from jax import lax
from jax.sharding import Mesh
from jax.sharding import PartitionSpec as P

COL = ("col_0", "col_1", "col_2")
ROW = ("row_0", "row_1")
ROW_COL = ("row_0", "row_1", "col_0", "col_1", "col_2")


def copy_for_each(x, axis):
    copies = jnp.broadcast_to(x, (lax.axis_size(axis), *x.shape))
    return lax.all_to_all(copies, axis, split_axis=0, concat_axis=0, tiled=True)


def in_order(pieces, dim):
    dims = list(pieces.shape[1:])
    dims[dim] *= pieces.shape[0]
    return jnp.moveaxis(pieces, 0, dim).reshape(dims)


def gather_directly(x, axis, dim):
    pieces = copy_for_each(x, axis)
    return in_order(pieces, dim)


def cut_along(x, dim, devices):
    dims = x.shape
    pieces = x.reshape(*dims[:dim], devices, dims[dim] // devices, *dims[dim + 1 :])
    return jnp.moveaxis(pieces, dim, 0)


def sum_at_owner(x, axis, dim):
    devices = lax.axis_size(axis)
    pieces = lax.all_to_all(cut_along(x, dim, devices), axis, 0, 0, tiled=True)
    return jnp.sum(pieces, axis=0)


def over_axes(x, axes):
    return functools.reduce(lax.psum, axes, x)


def normalize(embed):
    full = embed.astype(jnp.float32)
    scale = lax.rsqrt(jnp.mean(full * full, axis=-1, keepdims=True) + 1e-06)
    full = full * scale
    return (full, scale, full.astype(jnp.bfloat16))


def backward_norm(dnorm, full, scale):
    return scale * (dnorm - full * jnp.mean(dnorm * full, axis=-1, keepdims=True))


def tile_terms(
    source_count,
    source_region,
    source_subset,
    target_count,
    target_region,
    target_overall,
    sharpness_coefficient,
    shift_amount,
):
    similarity_value = jnp.dot(source_count, target_count.T, preferred_element_type=jnp.float32)
    pair_affinity = sharpness_coefficient * similarity_value + shift_amount
    positive = source_subset[:, None] == target_overall[None, :]
    retain_mask = positive | (source_region[:, None] != target_region[None, :])
    polarity_value = jnp.where(positive, 1.0, -1.0).astype(jnp.float32)
    partial_loss = jnp.sum(
        jnp.where(retain_mask, -jax.nn.log_sigmoid(polarity_value * pair_affinity), 0.0)
    )
    pairwise_slope = (
        jnp.where(
            retain_mask, -polarity_value * jax.nn.sigmoid(-polarity_value * pair_affinity), 0.0
        )
        * sharpness_coefficient
    ).astype(jnp.bfloat16)
    image_embed_gradient = jnp.dot(pairwise_slope, target_count, preferred_element_type=jnp.float32)
    param_d = lax.dot_general(
        pairwise_slope, source_count, (((0,), (0,)), ((), ())), preferred_element_type=jnp.float32
    )
    return (partial_loss, image_embed_gradient, param_d)


def on_device(
    lensed_picture_vectors,
    theta_feature_vectors,
    prior_domain_label,
    matched_theta_index,
    affinity_gain,
    affinity_shift,
):
    shard = lensed_picture_vectors.shape[0]
    hidden_size = lensed_picture_vectors.shape[1]
    col_count = lax.axis_size(COL)
    row_count = lax.axis_size(ROW)
    col_index = lax.axis_index(COL)
    sharpness_coefficient = affinity_gain[0] / hidden_size
    shift_amount = affinity_shift[0]
    data_full, data_scale, data_norm = normalize(lensed_picture_vectors)
    param_full, param_scale, param_norm = normalize(theta_feature_vectors)
    col_total = shard * row_count
    target_count, target_region = (
        gather_directly(param_norm, ROW, 0),
        gather_directly(prior_domain_label, ROW, 0),
    )
    place = jnp.arange(col_total, dtype=jnp.int32)
    target_overall = place // shard * (shard * col_count) + col_index * shard + place % shard
    source_count = lax.all_gather(data_norm, COL, axis=0, tiled=True)
    source_region = lax.all_gather(prior_domain_label, COL, axis=0, tiled=True)
    source_subset = lax.all_gather(matched_theta_index, COL, axis=0, tiled=True)
    partial_loss, image_embed_gradient, param_d = tile_terms(
        source_count,
        source_region,
        source_subset,
        target_count,
        target_region,
        target_overall,
        sharpness_coefficient,
        shift_amount,
    )
    data_dnorm = lax.psum_scatter(image_embed_gradient, COL, scatter_dimension=0, tiled=True)
    param_dnorm = sum_at_owner(param_d, ROW, 0)
    total = over_axes(partial_loss, ROW_COL)
    pair_total = shard * row_count * col_count
    loss = (total / (pair_total * pair_total)).reshape(1)
    grad_data = backward_norm(data_dnorm, data_full, data_scale)
    grad_param = backward_norm(param_dnorm, param_full, param_scale)
    return (loss, grad_data, grad_param)


def solution(mesh):
    torus = Mesh(mesh.devices.reshape(2, 4, 4, 2, 2), ("row_0", "row_1", "col_0", "col_1", "col_2"))
    in_specs = (P(ROW_COL, None), P(ROW_COL, None), P(ROW_COL), P(ROW_COL), P(), P())
    out_specs = (P(), P(ROW_COL, None), P(ROW_COL, None))
    return jax.shard_map(
        on_device, mesh=torus, in_specs=in_specs, out_specs=out_specs, check_vma=False
    )
```

profile of v0, /device:TPU:0, one launch (start us, length us, event | category | flops | bytes accessed | tf_op | source)
XLA Modules:
  0.0 257.8 jit_solution(16364265598439123908)
XLA Ops:
  7.2 0.0 all-gather.2.cloned.1.call-start
  7.2 1.0 fusion.19
  8.3 1.7 fusion.15
  10.0 0.0 all-gather.2.cloned.1.call-update
  10.0 1.3 broadcast_in_dim.24
  11.3 6.4 %all-to-all-start = ((s32[8,1,192]{2,1,0:T(1,128)}), s32[8,1,192]{2,1,0:T(1,128)S(1)}, u32[]{:S(2)}, u32[]{:S(2)}) async-start(s32[8,1,192]{2,1,0:T(1,128)} %broadcast_in_dim.24), calls=%async_computation | async-start | bytes 16384 | tf_op jit(solution)/shard_map/all_to_all | solution.py:16
  17.6 1.1 fusion.23
  18.7 1.0 fusion.12
  19.7 4.1 %all-to-all-done = s32[8,1,192]{2,1,0:T(1,128)S(1)} async-done(((s32[8,1,192]{2,1,0:T(1,128)}), s32[8,1,192]{2,1,0:T(1,128)S(1)}, u32[]{:S(2)}, u32[]{:S(2)}) %all-to-all-start) | async-done | bytes 6176 | tf_op jit(solution)/shard_map/all_to_all | solution.py:16
  23.8 1.3 broadcast_in_dim.27
  25.1 3.6 %all-to-all-start.1 = ((bf16[8,192,512]{2,1,0:T(8,128)(2,1)}), bf16[8,192,512]{2,1,0:T(8,128)(2,1)S(1)}, u32[]{:S(2)}, u32[]{:S(2)}) async-start(bf16[8,192,512]{2,1,0:T(8,128)(2,1)} %broadcast_in_dim.27), calls=%async_computation.1 | async-start | bytes 3145728 | tf_op jit(solution)/shard_map/all_to_all | solution.py:16
  28.7 0.0 reduce-scatter.2.cloned.1.call-start
  30.1 1.2 dynamic-slice
  32.0 0.9 dynamic-update-slice.1
  32.9 0.9 dynamic-update-slice
  33.7 74.2 %all-reduce.2 = (s32[3072]{0:T(1024)S(1)}, s32[3072]{0:T(1024)S(1)}) all-reduce(s32[3072]{0:T(1024)S(1)} %dynamic-update-slice.1, s32[3072]{0:T(1024)S(1)} %dynamic-update-slice), channel_id=1, replica_groups=mesh['row_0'=2,'row_1'=4,'col_0'=4,'col_1'=2,'col_2'=2] {'col_0','col_1'..., use_global_device_ids=true, to_apply=%add.1 | all-reduce | flops 6144 | bytes 49152
  108.0 0.1 ne.62
  108.0 0.0 all-to-all-done.1
  108.0 0.0 all-gather.2.cloned.1.call-done
  108.0 28.8 %multiply_convert_fusion = (bf16[3072,1536]{1,0:T(8,128)(2,1)S(1)}, f32[]{:T(128)}) fusion(f32[]{:T(128)} %bitcast.12, f32[]{:T(128)} %bitcast.1, s32[1536]{0:T(1024)S(1)} %ne.62, s32[1536]{0:T(1024)S(1)} %fusion.32, s32[3072]{0:T(1024)S(1)} %get-tuple-element.3, s32[3072]{0:T(1024)S(1)} %get-tuple-element.4, ...), kind=kOutput, calls=%fused_computation.14 | convolution fusion | flops 4949803008 | bytes 14192652 | tf_op jit(solution)/shard_map/dot_general | solution.py:67
  136.8 0.0 copy-start
  136.8 3.6 %copy-done = bf16[3072,1536]{1,0:T(8,128)(2,1)} copy-done((bf16[3072,1536]{1,0:T(8,128)(2,1)}, bf16[3072,1536]{1,0:T(8,128)(2,1)S(1)}, u32[]{:S(2)}) %copy-start) | copy-done | bytes 9437208
  140.5 6.9 %fusion.34 = f32[3072,512]{1,0:T(8,128)} fusion(bf16[3072,1536]{1,0:T(8,128)(2,1)S(1)} %get-tuple-element.5, bf16[1536,512]{1,0:T(8,128)(2,1)S(1)} %bitcast.15), kind=kOutput, calls=%fused_computation.52 | convolution fusion | flops 4831838208 | bytes 17301504 | tf_op jit(solution)/shard_map/dot_general | solution.py:81
  147.4 0.0 reduce-scatter.2.cloned.1.call-update
  147.4 10.7 %fusion.35 = f32[1536,512]{1,0:T(8,128)} fusion(bf16[3072,1536]{1,0:T(8,128)(2,1)} %copy-done, bf16[3072,512]{1,0:T(8,128)(2,1)} %all-gather.2.cloned.1.call-done), kind=kOutput, calls=%fused_computation.53 | convolution fusion | flops 4831838208 | bytes 15728640 | tf_op jit(solution)/shard_map/dot_general | solution.py:82
  158.1 5.3 %all-to-all-start.2 = ((f32[8,192,512]{2,1,0:T(8,128)}), f32[8,192,512]{2,1,0:T(8,128)S(1)}, u32[]{:S(2)}, u32[]{:S(2)}) async-start(f32[8,192,512]{2,1,0:T(8,128)} %bitcast.13), calls=%async_computation.3 | async-start | bytes 6291456 | tf_op jit(solution)/shard_map/all_to_all | solution.py:38
  163.4 48.4 %psum.35 = f32[]{:T(128)} all-reduce(f32[]{:T(128)} %get-tuple-element.6), channel_id=1, replica_groups=mesh['row_0'=2,'row_1'=4,'col_0'=4,'col_1'=2,'col_2'=2] {'row_0'}, use_global_device_ids=true, to_apply=%region_3.4 | all-reduce | flops 1 | bytes 8 | tf_op jit(solution)/shard_map/psum | solution.py:43
  211.8 11.0 %psum.36 = f32[]{:T(128)} all-reduce(f32[]{:T(128)} %psum.35), channel_id=1, replica_groups=mesh['row_0'=2,'row_1'=4,'col_0'=4,'col_1'=2,'col_2'=2] {'row_1'}, use_global_device_ids=true, to_apply=%region_4.5 | all-reduce | flops 1 | bytes 8 | tf_op jit(solution)/shard_map/psum | solution.py:43
  222.8 8.3 %psum.37 = f32[]{:T(128)} all-reduce(f32[]{:T(128)} %psum.36), channel_id=1, replica_groups=mesh['row_0'=2,'row_1'=4,'col_0'=4,'col_1'=2,'col_2'=2] {'col_0'}, use_global_device_ids=true, to_apply=%region_5.6 | all-reduce | flops 1 | bytes 8 | tf_op jit(solution)/shard_map/psum | solution.py:43
  231.2 7.0 %psum.38 = f32[]{:T(128)} all-reduce(f32[]{:T(128)} %psum.37), channel_id=1, replica_groups=mesh['row_0'=2,'row_1'=4,'col_0'=4,'col_1'=2,'col_2'=2] {'col_1'}, use_global_device_ids=true, to_apply=%region_6.7 | all-reduce | flops 1 | bytes 8 | tf_op jit(solution)/shard_map/psum | solution.py:43
  238.2 3.1 %psum.39 = f32[]{:T(128)} all-reduce(f32[]{:T(128)} %psum.38), channel_id=1, replica_groups=mesh['row_0'=2,'row_1'=4,'col_0'=4,'col_1'=2,'col_2'=2] {'col_2'}, use_global_device_ids=true, to_apply=%region_7.8 | all-reduce | flops 1 | bytes 8 | tf_op jit(solution)/shard_map/psum | solution.py:43
  241.9 0.0 all-to-all-done.2
  241.9 0.3 reduce_sum.58
  242.3 1.1 fusion.20
  243.5 1.8 fusion.22
  245.3 1.3 reduce-scatter.2.cloned.1.call-done
  246.6 1.2 fusion.16
  247.9 1.9 fusion.18
  (8 shorter events, 0.1 us)
Async XLA Ops:
  7.2 100.9 %all-gather.2.cloned.1.call-start = ((), (), s32[]{:S(2)}) async-start(), calls=%async_computation.4 | async-start | bytes 3342336 | tf_op jit(solution)/shard_map/all_gather | solution.py:112
  11.3 12.5 %all-to-all-start = ((s32[8,1,192]{2,1,0:T(1,128)}), s32[8,1,192]{2,1,0:T(1,128)S(1)}, u32[]{:S(2)}, u32[]{:S(2)}) async-start(s32[8,1,192]{2,1,0:T(1,128)} %broadcast_in_dim.24), calls=%async_computation | async-start | bytes 16384 | tf_op jit(solution)/shard_map/all_to_all | solution.py:16
  25.1 82.9 %all-to-all-start.1 = ((bf16[8,192,512]{2,1,0:T(8,128)(2,1)}), bf16[8,192,512]{2,1,0:T(8,128)(2,1)S(1)}, u32[]{:S(2)}, u32[]{:S(2)}) async-start(bf16[8,192,512]{2,1,0:T(8,128)(2,1)} %broadcast_in_dim.27), calls=%async_computation.1 | async-start | bytes 3145728 | tf_op jit(solution)/shard_map/all_to_all | solution.py:16
  28.7 217.9 %reduce-scatter.2.cloned.1.call-start = ((), (), s32[]{:S(2)}) async-start(), calls=%async_computation.5 | async-start | bytes 6684672 | tf_op jit(solution)/shard_map/reduce_scatter | solution.py:125
  136.8 3.6 %copy-start = (bf16[3072,1536]{1,0:T(8,128)(2,1)}, bf16[3072,1536]{1,0:T(8,128)(2,1)S(1)}, u32[]{:S(2)}) copy-start(bf16[3072,1536]{1,0:T(8,128)(2,1)S(1)} %get-tuple-element.5) | copy-start | bytes 28311556
  158.1 83.9 %all-to-all-start.2 = ((f32[8,192,512]{2,1,0:T(8,128)}), f32[8,192,512]{2,1,0:T(8,128)S(1)}, u32[]{:S(2)}, u32[]{:S(2)}) async-start(f32[8,192,512]{2,1,0:T(8,128)} %bitcast.13), calls=%async_computation.3 | async-start | bytes 6291456 | tf_op jit(solution)/shard_map/all_to_all | solution.py:38
Sparse Core Ops, SparseCore 0:
  11.0 53.3 all-gather.1
  147.5 99.0 reduce-scatter.1
where the time goes:
time: 259 us; the launch traced here: 258 us
  blocking collectives  152 us (59%)
  matrix products  46.4 us (18%)
  between operations  17.9 us (7%)
  starting transfers between devices  15.3 us (6%)
  other arithmetic  11.4 us (4%)
  local copies, waits for them, and re-layouts  9.29 us (4%)
  waiting for transfers between devices  5.47 us (2%)
    psum x5, blocking collectives, over_axes(): return functools.reduce(lax.psum, axes, x)  77.9 us
    unnamed x1, blocking collectives  74.2 us
    dot_general x1, matrix products, tile_terms(): jnp.dot(source_count, target_count.T, preferred_element_type=jnp.float32)  28.8 us
    dot_general x1, matrix products, tile_terms(): lax.dot_general(pairwise_slope, source_count, (((0,), (0,)), ((), ())), p...  10.7 us
    all_to_all x2, starting transfers between devices, copy_for_each(): return lax.all_to_all(copies, axis, split_axis=0, concat_axis=0, tiled=True)  9.93 us
    dot_general x1, matrix products, tile_terms(): jnp.dot(pairwise_slope, target_count, preferred_element_type=jnp.float32)  6.91 us
    unnamed x7, local copies, waits for them, and re-layouts  6.64 us
    all_to_all x1, starting transfers between devices, sum_at_owner(): pieces = lax.all_to_all(cut_along(x, dim, devices), axis, 0, 0, tiled=True)  5.33 us
  transfers between devices with their start and end apart: 5, of which 2 were waited for; matrix products, arithmetic and copies ran while one was open for 8% of the time, Pallas kernels for 0%

commit v1 on v0

--- a/solution.py
+++ b/solution.py
@@ -40,7 +40,7 @@
 
 
 def over_axes(x, axes):
-    return functools.reduce(lax.psum, axes, x)
+    return lax.psum(x, axes)
 
 
 def normalize(embed):
@@ -110,8 +110,9 @@
     place = jnp.arange(col_total, dtype=jnp.int32)
     target_overall = place // shard * (shard * col_count) + col_index * shard + place % shard
     source_count = lax.all_gather(data_norm, COL, axis=0, tiled=True)
-    source_region = lax.all_gather(prior_domain_label, COL, axis=0, tiled=True)
-    source_subset = lax.all_gather(matched_theta_index, COL, axis=0, tiled=True)
+    packed = gather_directly(matched_theta_index * 64 + prior_domain_label, COL, 0)
+    source_region = packed & 63
+    source_subset = packed >> 6
     partial_loss, image_embed_gradient, param_d = tile_terms(
         source_count,
         source_region,

time: 259 us -> 254 us (0.981)
  blocking collectives: 152 us -> 111 us
  waiting for transfers between devices: 5.47 us -> 38.1 us
  starting transfers between devices: 15.3 us -> 21.2 us
    unnamed x1 -> x0, blocking collectives: 74.2 us -> none
    all_to_all x2 -> x3, waiting for transfers between devices: 4.1 us -> 37.2 us  [copy_for_each(): return lax.all_to_all(copies, axis, split_axis=0, concat_axis=0, tiled=True)]
    psum x5 -> x1, blocking collectives: 77.9 us -> 111 us  [over_axes(): return lax.psum(x, axes)]
    all_to_all x2 -> x3, starting transfers between devices: 9.93 us -> 16.7 us  [copy_for_each(): return lax.all_to_all(copies, axis, split_axis=0, concat_axis=0, tiled=True)]
    unnamed x7 -> x2, local copies, waits for them, and re-layouts: 6.64 us -> 3.62 us
  transfers between devices with their start and end apart: 5 -> 6, of which waited for: 2 -> 4; matrix products, arithmetic and copies ran while one was open for 8% -> 8% of each run, Pallas kernels for 0% -> 0%
where the time goes in v1:
time: 254 us; the launch traced here: 253 us
  blocking collectives  111 us (44%)
  matrix products  46.4 us (18%)
  waiting for transfers between devices  38.1 us (15%)
  starting transfers between devices  21.2 us (8%)
  between operations  17.2 us (7%)
  other arithmetic  12.2 us (5%)
  local copies, waits for them, and re-layouts  7.03 us (3%)
    psum x1, blocking collectives, over_axes(): return lax.psum(x, axes)  111 us
    all_to_all x3, waiting for transfers between devices, copy_for_each(): return lax.all_to_all(copies, axis, split_axis=0, concat_axis=0, tiled=True)  37.2 us
    dot_general x1, matrix products, tile_terms(): jnp.dot(source_count, target_count.T, preferred_element_type=jnp.float32)  28.8 us
    all_to_all x3, starting transfers between devices, copy_for_each(): return lax.all_to_all(copies, axis, split_axis=0, concat_axis=0, tiled=True)  16.7 us
    dot_general x1, matrix products, tile_terms(): lax.dot_general(pairwise_slope, source_count, (((0,), (0,)), ((), ())), p...  10.7 us
    dot_general x1, matrix products, tile_terms(): jnp.dot(pairwise_slope, target_count, preferred_element_type=jnp.float32)  6.9 us
  transfers between devices with their start and end apart: 6, of which 4 were waited for; matrix products, arithmetic and copies ran while one was open for 8% of the time, Pallas kernels for 0%

profile of v1, /device:TPU:0, one launch (start us, length us, event | category | flops | bytes accessed | tf_op | source)
XLA Modules:
  0.0 252.9 jit_solution(1417830082828834079)
XLA Ops:
  7.2 0.0 all-gather.2.cloned.1.call-start
  7.2 1.0 fusion.19
  8.3 1.7 fusion.15
  10.0 0.0 all-gather.2.cloned.1.call-update
  10.0 1.3 broadcast_in_dim.28
  11.3 6.4 %all-to-all-start.1 = ((s32[8,1,192]{2,1,0:T(1,128)}), s32[8,1,192]{2,1,0:T(1,128)S(1)}, u32[]{:S(2)}, u32[]{:S(2)}) async-start(s32[8,1,192]{2,1,0:T(1,128)} %broadcast_in_dim.28), calls=%async_computation.1 | async-start | bytes 16384 | tf_op jit(solution)/shard_map/all_to_all | solution.py:16
  17.6 1.1 fusion.23
  18.7 0.7 multiply_add_fusion.1
  19.4 4.4 %all-to-all-done.1 = s32[8,1,192]{2,1,0:T(1,128)S(1)} async-done(((s32[8,1,192]{2,1,0:T(1,128)}), s32[8,1,192]{2,1,0:T(1,128)S(1)}, u32[]{:S(2)}, u32[]{:S(2)}) %all-to-all-start.1) | async-done | bytes 6176 | tf_op jit(solution)/shard_map/all_to_all | solution.py:16
  23.8 0.6 broadcast_in_dim.27
  24.4 6.7 %all-to-all-start = ((s32[16,1,192]{2,1,0:T(1,128)}), s32[16,1,192]{2,1,0:T(1,128)S(1)}, u32[]{:S(2)}, u32[]{:S(2)}) async-start(s32[16,1,192]{2,1,0:T(1,128)} %broadcast_in_dim.27), calls=%async_computation | async-start | bytes 32768 | tf_op jit(solution)/shard_map/all_to_all | solution.py:16
  31.2 1.0 fusion.12
  32.2 6.6 %all-to-all-done = s32[16,1,192]{2,1,0:T(1,128)S(1)} async-done(((s32[16,1,192]{2,1,0:T(1,128)}), s32[16,1,192]{2,1,0:T(1,128)S(1)}, u32[]{:S(2)}, u32[]{:S(2)}) %all-to-all-start) | async-done | bytes 12320 | tf_op jit(solution)/shard_map/all_to_all | solution.py:16
  38.8 1.3 broadcast_in_dim.31
  40.1 3.6 %all-to-all-start.2 = ((bf16[8,192,512]{2,1,0:T(8,128)(2,1)}), bf16[8,192,512]{2,1,0:T(8,128)(2,1)S(1)}, u32[]{:S(2)}, u32[]{:S(2)}) async-start(bf16[8,192,512]{2,1,0:T(8,128)(2,1)} %broadcast_in_dim.31), calls=%async_computation.2 | async-start | bytes 3145728 | tf_op jit(solution)/shard_map/all_to_all | solution.py:16
  43.7 0.0 reduce-scatter.2.cloned.1.call-start
  45.1 0.1 ne.62
  45.1 0.1 shift-right-arithmetic_reduce_fusion
  45.2 0.1 and.36
  45.3 0.1 shift_right_arithmetic.15
  45.4 26.2 %all-to-all-done.2 = bf16[8,192,512]{2,1,0:T(8,128)(2,1)S(1)} async-done(((bf16[8,192,512]{2,1,0:T(8,128)(2,1)}), bf16[8,192,512]{2,1,0:T(8,128)(2,1)S(1)}, u32[]{:S(2)}, u32[]{:S(2)}) %all-to-all-start.2) | async-done | bytes 1572896 | tf_op jit(solution)/shard_map/all_to_all | solution.py:16
  71.6 0.8 all-gather.2.cloned.1.call-done
  72.5 28.8 %multiply_convert_fusion = (bf16[3072,1536]{1,0:T(8,128)(2,1)S(1)}, f32[]{:T(128)}) fusion(f32[]{:T(128)} %bitcast.11, f32[]{:T(128)} %bitcast, s32[1536]{0:T(1024)S(1)} %ne.62, s32[1536]{0:T(1024)S(1)} %fusion.32, s32[3072]{0:T(1024)S(1)} %and.36, s32[3072]{0:T(1024)S(1)} %shift_right_arithmetic.15, bf16[3072,512]{1,0:T(8,128)(2,1)} %all-gather.2.cloned.1.call-done, ...), kind=kOutput, calls=%fused_computation.14 | convolution fusion | flops 4949803008 | bytes 14192652 | tf_op jit(solution)/shard_map/dot_general | solution.py:67
  101.3 0.0 copy-start
  101.3 3.6 %copy-done = bf16[3072,1536]{1,0:T(8,128)(2,1)} copy-done((bf16[3072,1536]{1,0:T(8,128)(2,1)}, bf16[3072,1536]{1,0:T(8,128)(2,1)S(1)}, u32[]{:S(2)}) %copy-start) | copy-done | bytes 9437208
  104.9 6.9 %fusion.34 = f32[3072,512]{1,0:T(8,128)} fusion(bf16[3072,1536]{1,0:T(8,128)(2,1)S(1)} %get-tuple-element.5, bf16[1536,512]{1,0:T(8,128)(2,1)S(1)} %bitcast.14), kind=kOutput, calls=%fused_computation.55 | convolution fusion | flops 4831838208 | bytes 17301504 | tf_op jit(solution)/shard_map/dot_general | solution.py:81
  111.8 0.0 reduce-scatter.2.cloned.1.call-update
  111.8 10.7 %fusion.35 = f32[1536,512]{1,0:T(8,128)} fusion(bf16[3072,1536]{1,0:T(8,128)(2,1)} %copy-done, bf16[3072,512]{1,0:T(8,128)(2,1)} %all-gather.2.cloned.1.call-done), kind=kOutput, calls=%fused_computation.56 | convolution fusion | flops 4831838208 | bytes 15728640 | tf_op jit(solution)/shard_map/dot_general | solution.py:82
  122.5 4.4 %all-to-all-start.3 = ((f32[8,192,512]{2,1,0:T(8,128)}), f32[8,192,512]{2,1,0:T(8,128)S(1)}, u32[]{:S(2)}, u32[]{:S(2)}) async-start(f32[8,192,512]{2,1,0:T(8,128)} %bitcast.12), calls=%async_computation.4 | async-start | bytes 6291456 | tf_op jit(solution)/shard_map/all_to_all | solution.py:38
  126.9 110.8 %psum.7 = f32[]{:T(128)} all-reduce(f32[]{:T(128)} %get-tuple-element.6), channel_id=1, replica_groups=mesh['row_0'=2,'row_1'=4,'col_0'=4,'col_1'=2,'col_2'=2] {'row_0','row_1'..., use_global_device_ids=true, to_apply=%region_3.4 | all-reduce | flops 1 | bytes 8 | tf_op jit(solution)/shard_map/psum | solution.py:43
  238.4 0.0 all-to-all-done.3
  238.4 0.3 reduce_sum.58
  238.8 1.1 fusion.20
  239.9 1.8 fusion.22
  241.8 0.0 reduce-scatter.2.cloned.1.call-done
  241.8 1.2 fusion.16
  243.0 1.9 fusion.18
  (6 shorter events, 0.1 us)
Async XLA Ops:
  7.2 65.3 %all-gather.2.cloned.1.call-start = ((), (), s32[]{:S(2)}) async-start(), calls=%async_computation.5 | async-start | bytes 3342336 | tf_op jit(solution)/shard_map/all_gather | solution.py:112
  11.3 12.5 %all-to-all-start.1 = ((s32[8,1,192]{2,1,0:T(1,128)}), s32[8,1,192]{2,1,0:T(1,128)S(1)}, u32[]{:S(2)}, u32[]{:S(2)}) async-start(s32[8,1,192]{2,1,0:T(1,128)} %broadcast_in_dim.28), calls=%async_computation.1 | async-start | bytes 16384 | tf_op jit(solution)/shard_map/all_to_all | solution.py:16
  24.4 14.3 %all-to-all-start = ((s32[16,1,192]{2,1,0:T(1,128)}), s32[16,1,192]{2,1,0:T(1,128)S(1)}, u32[]{:S(2)}, u32[]{:S(2)}) async-start(s32[16,1,192]{2,1,0:T(1,128)} %broadcast_in_dim.27), calls=%async_computation | async-start | bytes 32768 | tf_op jit(solution)/shard_map/all_to_all | solution.py:16
  40.1 31.5 %all-to-all-start.2 = ((bf16[8,192,512]{2,1,0:T(8,128)(2,1)}), bf16[8,192,512]{2,1,0:T(8,128)(2,1)S(1)}, u32[]{:S(2)}, u32[]{:S(2)}) async-start(bf16[8,192,512]{2,1,0:T(8,128)(2,1)} %broadcast_in_dim.31), calls=%async_computation.2 | async-start | bytes 3145728 | tf_op jit(solution)/shard_map/all_to_all | solution.py:16
  43.7 198.1 %reduce-scatter.2.cloned.1.call-start = ((), (), s32[]{:S(2)}) async-start(), calls=%async_computation.6 | async-start | bytes 6684672 | tf_op jit(solution)/shard_map/reduce_scatter | solution.py:126
  101.3 3.6 %copy-start = (bf16[3072,1536]{1,0:T(8,128)(2,1)}, bf16[3072,1536]{1,0:T(8,128)(2,1)S(1)}, u32[]{:S(2)}) copy-start(bf16[3072,1536]{1,0:T(8,128)(2,1)S(1)} %get-tuple-element.5) | copy-start | bytes 28311556
  122.5 115.9 %all-to-all-start.3 = ((f32[8,192,512]{2,1,0:T(8,128)}), f32[8,192,512]{2,1,0:T(8,128)S(1)}, u32[]{:S(2)}, u32[]{:S(2)}) async-start(f32[8,192,512]{2,1,0:T(8,128)} %bitcast.12), calls=%async_computation.4 | async-start | bytes 6291456 | tf_op jit(solution)/shard_map/all_to_all | solution.py:38
Sparse Core Ops, SparseCore 0:
  11.0 61.4 all-gather.1
  111.9 102.6 reduce-scatter.1

commit v2 on v0

v2 whole, which is shorter than its diff:
```python
import jax
import jax.numpy as jnp
from jax import lax
from jax.experimental import pallas as pl
from jax.experimental.pallas import tpu as pltpu
from jax.sharding import PartitionSpec as P

f32 = jnp.float32
bf16 = jnp.bfloat16
i32 = jnp.int32
LOG2E = 1.4426950408889634
LN2 = 0.6931471805599453
MASKED = -1e5
NT = (((1,), (1,)), ((), ()))
NN = (((1,), (0,)), ((), ()))
TN = (((0,), (0,)), ((), ()))
MESH = pl.DeviceIdType.MESH
B = 192
E = 512
V = 4 * B
XU = [(0, 0), (0, 1), (3, 0), (1, 0), (3, 1), (1, 1), (2, 0), (2, 1)]
PZ = [3, 1, 0, 2]
N_GATHER = 22
N_SEM = 2 * N_GATHER + 8 + 14 + 7


def xs(ry, rx, rc=0):
    return 2 * XU.index((ry, rx)) + rc


def ps(rz, rx):
    return 2 * PZ.index(rz) + rx


def rows(slot):
    return pl.ds(slot * B, B)


def pair_terms(s, row_region, row_match, col_region, col_index, gain, gain2, shift2):
    t = s * gain2 + shift2
    positive = row_match == col_index
    t = jnp.where(positive, -t, jnp.where(row_region != col_region, t, MASKED))
    soft = jnp.log2(1.0 + jnp.exp2(t))
    slope = jnp.exp2(t - soft) * jnp.where(positive, -gain, gain)
    return slope.astype(bf16), soft


def fold(x):
    return jnp.sum(x.reshape(x.shape[0] // 8, 8, 128), axis=0)


def kernel(
    gain_ref, shift_ref, x_ref, p_ref, lab_ref,
    loss_ref, gx_ref, gp_ref,
    xb, pb, lx, lp, rr, rm, cr, cj, dx, dp, rc, ry, rz, acc, lsend, lrecv, send_sem, recv_sem,
):
    r, c = lax.axis_index("row"), lax.axis_index("col")
    xl, z = r // 4, r % 4
    y, xh, core = c // 4, (c // 2) % 2, c % 2
    low = c % 4
    cp = (r, c + 1 - 2 * core)
    dxp = ((1 - xl) * 4 + z, c)
    pxp = ((1 - xl) * 4 + z, y * 4 + (1 - xh) * 2 + core)
    yu, yd = (r, ((y + 1) % 4) * 4 + low), (r, ((y + 3) % 4) * 4 + low)
    zu, zd = (xl * 4 + (z + 1) % 4, c), (xl * 4 + (z + 3) % 4, c)

    count = [0]
    pending = []

    def send(src, dst, device):
        k = count[0]
        count[0] += 1
        copy = pltpu.make_async_remote_copy(
            src_ref=src, dst_ref=dst, send_sem=send_sem.at[k], recv_sem=recv_sem.at[k],
            device_id=device, device_id_type=MESH,
        )
        copy.start()
        pending.append(copy)
        return copy

    def normalize(ref):
        full = ref[...].astype(f32)
        scale = lax.rsqrt(jnp.mean(full * full, axis=-1, keepdims=True) + 1e-06)
        return full * scale, scale

    barrier = pltpu.get_barrier_semaphore()
    for peer in (cp, dxp, pxp, yu, yd, zu, zd):
        pl.semaphore_signal(barrier, inc=1, device_id=peer, device_id_type=MESH)
    own_x, own_p = xs(0, 0), ps(0, 0)
    xb[rows(own_x), :] = normalize(x_ref)[0].astype(bf16)
    pb[rows(own_p), :] = normalize(p_ref)[0].astype(bf16)
    lx[own_x] = lab_ref[0, :, 0:256]
    lp[own_p] = lab_ref[0]
    pl.semaphore_wait(barrier, 7)

    got = {}

    def send_x(src, dst, device):
        label = lab_ref.at[0, :, pl.ds(0, 256)] if src == own_x else lx.at[src]
        got["x", dst] = (send(label, lx.at[dst], device), send(xb.at[rows(src)], xb.at[rows(dst)], device))

    def send_p(src, dst, device):
        label = lab_ref.at[0] if src == own_p else lp.at[src]
        got["p", dst] = (send(label, lp.at[dst], device), send(pb.at[rows(src)], pb.at[rows(dst)], device))

    def wait(kind, slot):
        for copy in got[kind, slot]:
            copy.wait_recv()

    def row_info(slot):
        t = jnp.transpose(jnp.broadcast_to(lx[slot], (128, 256)))[0:B]
        rr[rows(slot), :] = t & 63
        rm[rows(slot), :] = t >> 6

    def col_info(rz_):
        first, second = lp[ps(rz_, 0)], lp[ps(rz_, 1)]
        zz = (z + rz_) % 4
        base0 = ((xl * 4 + zz) * 16 + y * 4 + xh * 2 + core) * B
        base1 = (((1 - xl) * 4 + zz) * 16 + y * 4 + (1 - xh) * 2 + core) * B
        lane = lax.broadcasted_iota(i32, (1, 128), 1)
        off = ps(rz_, 0) * B
        parts = (first[:, 0:128], first[:, 128:256] + second[:, 256:384], second[:, 384:512])
        for k in range(3):
            at = lane + k * 128
            cr[:, off + k * 128 : off + (k + 1) * 128] = parts[k] & 63
            cj[:, off + k * 128 : off + (k + 1) * 128] = jnp.where(at < B, base0 + at, base1 + at - B)

    send_x(own_x, xs(0, 1), dxp)
    send_p(own_p, ps(0, 1), pxp)
    send_x(own_x, xs(3, 0), yu)
    send_x(own_x, xs(1, 0), yd)
    send_p(own_p, ps(3, 0), zu)
    send_p(own_p, ps(1, 0), zd)
    send_x(own_x, xs(0, 0, 1), cp)

    dx[...] = jnp.zeros_like(dx)
    dp[...] = jnp.zeros_like(dp)
    acc[...] = jnp.zeros_like(acc)
    row_info(own_x)
    gain = gain_ref[0] / E
    gain2 = gain * LOG2E
    shift2 = shift_ref[0] * LOG2E

    def tile(v, c0, width):
        r0 = pl.multiple_of(v * V, V)
        x = xb[pl.ds(r0, V), :]
        p = pb[pl.ds(c0, width), :]
        s = lax.dot_general(x, p, NT, preferred_element_type=f32)
        region, match = rr[pl.ds(r0, V), :], rm[pl.ds(r0, V), :]
        slopes, total = [], None
        for k in range(width // 128):
            cs = pl.ds(c0 + k * 128, 128)
            slope, soft = pair_terms(
                s[:, k * 128 : (k + 1) * 128], region, match, cr[:, cs], cj[:, cs], gain, gain2, shift2
            )
            slopes.append(slope)
            soft = fold(soft)
            total = soft if total is None else total + soft
        acc[...] += total
        g = jnp.concatenate(slopes, axis=1)
        dx[pl.ds(r0, V), :] += lax.dot_general(g, p, NN, preferred_element_type=f32)
        dp[pl.ds(c0, width), :] += lax.dot_general(g, x, TN, preferred_element_type=f32)

    def run(v0, n, c0, width):
        def body(i, _):
            tile(v0 + i, c0, width)
            return 0

        lax.fori_loop(0, n, body, 0)

    wait("x", xs(0, 1))
    send_x(xs(0, 1), xs(3, 1), yu)
    send_x(xs(0, 1), xs(1, 1), yd)
    send_x(xs(0, 1), xs(0, 1, 1), cp)
    wait("p", ps(0, 1))
    send_p(ps(0, 1), ps(3, 1), zu)
    send_p(ps(0, 1), ps(1, 1), zd)
    wait("x", xs(3, 0))
    send_x(xs(3, 0), xs(2, 0), yu)
    send_x(xs(3, 0), xs(3, 0, 1), cp)
    wait("x", xs(1, 0))
    send_x(xs(1, 0), xs(1, 0, 1), cp)
    wait("p", ps(3, 0))
    send_p(ps(3, 0), ps(2, 0), zu)
    wait("p", ps(1, 0))
    col_info(0)
    for u in ((0, 1), (3, 0), (1, 0)):
        row_info(xs(*u))
    for u in ((0, 0), (0, 1), (3, 0), (1, 0)):
        wait("x", xs(*u, 1))
        row_info(xs(*u, 1))
    run(0, 2, 2 * V // 2, V // 2)

    wait("x", xs(1, 1))
    send_x(xs(1, 1), xs(2, 1), yd)
    send_x(xs(1, 1), xs(1, 1, 1), cp)
    wait("p", ps(1, 1))
    send_p(ps(1, 1), ps(2, 1), zd)
    wait("x", xs(3, 1))
    send_x(xs(3, 1), xs(3, 1, 1), cp)
    wait("p", ps(3, 1))
    col_info(3)
    col_info(1)
    run(0, 2, 0, V)

    for u in ((2, 0), (2, 1)):
        wait("x", xs(*u))
        send_x(xs(*u), xs(*u, 1), cp)
    wait("p", ps(2, 0))
    wait("p", ps(2, 1))
    col_info(2)
    for u in ((3, 1), (1, 1)):
        row_info(xs(*u))
        wait("x", xs(*u, 1))
        row_info(xs(*u, 1))
    for u in ((2, 0), (2, 1)):
        row_info(xs(*u))
        wait("x", xs(*u, 1))
        row_info(xs(*u, 1))
    tile(3, V, V)
    tile(3, 0, V)

    half = {}

    def to_core(u):
        k = XU.index(u)
        half[u] = send(dx.at[rows(xs(*u, 1))], rc.at[k], cp)

    def add_core(u):
        half[u].wait_recv()
        dx[rows(xs(*u)), :] += rc[XU.index(u)]

    def send_dx(u, k, device):
        return send(dx.at[rows(xs(*u))], ry.at[k], device)

    def send_dp(u, k, device):
        return send(dp.at[rows(ps(*u))], rz.at[k], device)

    def add_dx(u, k, copy):
        copy.wait_recv()
        dx[rows(xs(*u)), :] += ry[k]

    def add_dp(u, k, copy):
        copy.wait_recv()
        dp[rows(ps(*u)), :] += rz[k]

    to_core((2, 0))
    to_core((2, 1))
    tile(0, 3 * V // 2, V // 2)
    add_core((2, 0))
    xa = send_dx((2, 0), 0, yd)
    add_core((2, 1))
    xb_ = send_dx((2, 1), 1, yu)
    tile(1, 3 * V // 2, V // 2)
    for u in ((0, 0), (0, 1), (3, 0), (1, 0)):
        to_core(u)
    tile(2, V, V)
    pa = send_dp((2, 0), 0, zd)
    pb_ = send_dp((2, 1), 1, zu)
    for u in ((0, 0), (0, 1), (3, 0), (1, 0)):
        add_core(u)
    tile(2, 0, V)
    to_core((3, 1))
    to_core((1, 1))

    lsend[0] = jnp.sum(acc[...], axis=0, keepdims=True)
    y1 = (r, (y + 1 - 2 * (y % 2)) * 4 + low)
    y2 = (r, (3 - y) * 4 + low)
    z1 = (xl * 4 + z + 1 - 2 * (z % 2), c)
    z2 = (xl * 4 + 3 - z, c)
    stages = [cp, dxp, pxp, y1, y2, z1, z2]
    exchange = [None] * 7

    def loss_send(k):
        exchange[k] = send(lsend.at[k], lrecv.at[k], stages[k])

    def loss_add(k):
        exchange[k].wait_recv()
        lsend[k + 1] = lsend[k] + lrecv[k]

    add_core((3, 1))
    xd = send_dx((3, 1), 3, yd)
    pd = send_dp((3, 1), 3, zd)
    add_core((1, 1))
    add_dx((1, 1), 1, xb_)
    xf = send_dx((1, 1), 5, yu)
    loss_send(0)
    add_dx((3, 0), 0, xa)
    xc = send_dx((3, 0), 2, yd)
    xe = send_dx((1, 0), 4, yu)
    loss_add(0)
    loss_send(1)
    add_dp((1, 1), 1, pb_)
    pf = send_dp((1, 1), 5, zu)
    pe = send_dp((1, 0), 4, zu)
    add_dp((3, 0), 0, pa)
    pc = send_dp((3, 0), 2, zd)
    loss_add(1)
    loss_send(2)
    add_dx((0, 1), 3, xd)
    loss_add(2)
    loss_send(3)
    add_dx((0, 1), 5, xf)
    xg = send_dx((0, 1), 6, dxp)
    loss_add(3)
    loss_send(4)
    add_dp((0, 1), 3, pd)
    add_dp((0, 1), 5, pf)
    pg = send_dp((0, 1), 6, pxp)
    loss_add(4)
    loss_send(5)
    add_dx((0, 0), 2, xc)
    add_dx((0, 0), 4, xe)
    loss_add(5)
    loss_send(6)
    add_dp((0, 0), 2, pc)
    add_dp((0, 0), 4, pe)
    loss_add(6)
    n = float(128 * B)
    loss_ref[0] = jnp.sum(lsend[7]) * LN2 / (n * n)

    def finish(ref, dnorm, out):
        full, scale = normalize(ref)
        out[...] = scale * (dnorm - full * jnp.mean(dnorm * full, axis=-1, keepdims=True))

    xg.wait_recv()
    finish(x_ref, dx[rows(own_x), :] + ry[6], gx_ref)
    pg.wait_recv()
    finish(p_ref, dp[rows(own_p), :] + rz[6], gp_ref)
    for copy in pending:
        copy.wait_send()
    assert count[0] == N_SEM


def on_device(lensed, theta, region, match, gain, shift):
    packed = match * 64 + region
    lab = jnp.concatenate([jnp.pad(packed, (0, 64)), jnp.pad(packed, (64, 0))]).reshape(1, 1, 512)
    vmem = pl.BlockSpec(memory_space=pltpu.VMEM)
    smem = pl.BlockSpec(memory_space=pltpu.SMEM)
    return pl.pallas_call(
        kernel,
        out_shape=(
            jax.ShapeDtypeStruct((1,), f32),
            jax.ShapeDtypeStruct((B, E), f32),
            jax.ShapeDtypeStruct((B, E), f32),
        ),
        in_specs=[smem, smem, vmem, vmem, vmem],
        out_specs=(smem, vmem, vmem),
        scratch_shapes=[
            pltpu.VMEM((16 * B, E), bf16),
            pltpu.VMEM((8 * B, E), bf16),
            pltpu.VMEM((16, 1, 256), i32),
            pltpu.VMEM((8, 1, 512), i32),
            pltpu.VMEM((16 * B, 128), i32),
            pltpu.VMEM((16 * B, 128), i32),
            pltpu.VMEM((1, 8 * B), i32),
            pltpu.VMEM((1, 8 * B), i32),
            pltpu.VMEM((16 * B, E), f32),
            pltpu.VMEM((8 * B, E), f32),
            pltpu.VMEM((8, B, E), f32),
            pltpu.VMEM((7, B, E), f32),
            pltpu.VMEM((7, B, E), f32),
            pltpu.VMEM((8, 128), f32),
            pltpu.VMEM((8, 1, 128), f32),
            pltpu.VMEM((7, 1, 128), f32),
            pltpu.SemaphoreType.DMA((N_SEM,)),
            pltpu.SemaphoreType.DMA((N_SEM,)),
        ],
        compiler_params=pltpu.CompilerParams(
            collective_id=0, has_side_effects=True, vmem_limit_bytes=60 << 20
        ),
        name="pairs",
    )(gain, shift, lensed, theta, lab)


def solution(mesh):
    both = ("row", "col")
    in_specs = (P(both, None), P(both, None), P(both), P(both), P(), P())
    out_specs = (P(), P(both, None), P(both, None))
    return jax.shard_map(
        on_device, mesh=mesh, in_specs=in_specs, out_specs=out_specs, check_vma=False
    )
```

time: 259 us -> 84.3 us (0.33)
  blocking collectives: 152 us -> 0 us
  Pallas kernels: 0 us -> 76.8 us
  matrix products: 46.4 us -> 0 us
  starting transfers between devices: 15.3 us -> 0 us
  between operations: 17.9 us -> 3.77 us
  other arithmetic: 11.4 us -> 0.66 us
  local copies, waits for them, and re-layouts: 9.29 us -> 2.58 us
  waiting for transfers between devices: 5.47 us -> 0 us
    psum x5 -> x0, blocking collectives: 77.9 us -> none  [over_axes(): return functools.reduce(lax.psum, axes, x)]
    pallas_call x0 -> x1, Pallas kernels: none -> 76.8 us  [on_device(): pl.pallas_call(kernel, out_shape=(jax.ShapeDtypeStruct((1,), f32), jax.Sh...]
    unnamed x1 -> x0, blocking collectives: 74.2 us -> none
    dot_general x3 -> x0, matrix products: 46.4 us -> none  [the longest x1 28.8 us: tile_terms(): jnp.dot(source_count, target_count.T, preferred_element_type=jnp.float32)]
    all_to_all x3 -> x0, starting transfers between devices: 15.3 us -> none  [the longest x2 9.93 us: copy_for_each(): return lax.all_to_all(copies, axis, split_axis=0, concat_axis=0, tiled=True)]
    reduce_sum x5 -> x0, other arithmetic: 4.83 us -> none  [the longest x2 2.38 us: backward_norm(): jnp.mean(dnorm * full, axis=-1, keepdims=True)]
    all_to_all x3 -> x0, waiting for transfers between devices: 4.11 us -> none  [the longest x2 4.1 us: copy_for_each(): return lax.all_to_all(copies, axis, split_axis=0, concat_axis=0, tiled=True)]
    unnamed x7 -> x8, local copies, waits for them, and re-layouts: 6.64 us -> 2.58 us
  transfers between devices with their start and end apart: 5 -> 0, of which waited for: 2 -> 0; matrix products, arithmetic and copies ran while one was open for 8% -> 0% of each run, Pallas kernels for 0% -> 0%
where the time goes in v2:
time: 84.3 us; the launch traced here: 83.8 us
  Pallas kernels  76.8 us (91%)
  between operations  3.77 us (4%)
  local copies, waits for them, and re-layouts  2.58 us (3%)
    pallas_call x1, Pallas kernels, on_device(): pl.pallas_call(kernel, out_shape=(jax.ShapeDtypeStruct((1,), f32), jax.Sh...  76.8 us
    unnamed x8, local copies, waits for them, and re-layouts  2.58 us

profile of v2, /device:TPU:0, one launch (start us, length us, event | category | flops | bytes accessed | tf_op | source)
XLA Modules:
  0.0 83.8 jit_solution(16008515944013974109)
XLA Ops:
  0.6 0.0 copy-start.2
  1.3 0.0 copy-start.1
  2.0 0.0 copy-done.2
  2.0 0.0 copy-done.1
  2.0 0.7 pad_add_fusion
  2.7 76.8 %pairs.1 = (f32[1]{0:T(128)}, f32[192,512]{1,0:T(8,128)}, f32[192,512]{1,0:T(8,128)}) custom-call(f32[1]{0:T(128)S(6)} %copy.12.gain_ref, f32[1]{0:T(128)S(6)} %copy.13.shift_ref, bf16[192,512]{1,0:T(8,128)(2,1)} %x_ref.1, bf16[192,512]{1,0:T(8,128)(2,1)} %p_ref.1, s32[1,1,512]{2,1,0:T(1,128)} %bitcast.1), custom_call_target="tpu_custom_call" | custom-call | tf_op jit(solution)/shard_map/pairs/pallas_call | solution.py:340
  80.1 0.0 copy-start
  80.1 1.8 %copy.15 = f32[192,512]{1,0:T(8,128)} copy(f32[192,512]{1,0:T(8,128)} %get-tuple-element.7) | data formatting | bytes 786432
  81.9 0.0 copy-done
  81.9 0.7 copy.16
  (1 shorter events, 0.0 us)
Async XLA Ops:
  0.6 1.3 %copy-start.2 = (s32[192]{0:T(256)S(1)}, s32[192]{0:T(256)}, u32[]{:S(2)}) copy-start(s32[192]{0:T(256)} %param.9) | copy-start | bytes 2308
  1.3 0.7 copy-start.1
  80.1 1.8 %copy-start = (f32[192,512]{1,0:T(8,128)S(1)}, f32[192,512]{1,0:T(8,128)}, u32[]{:S(2)}) copy-start(f32[192,512]{1,0:T(8,128)} %get-tuple-element.8) | copy-start | bytes 1179652

commit v3 on v2

v3 whole, which is shorter than its diff:
```python
import jax
import jax.numpy as jnp
from jax import lax
from jax.experimental import pallas as pl
from jax.experimental.pallas import tpu as pltpu
from jax.sharding import PartitionSpec as P

f32 = jnp.float32
bf16 = jnp.bfloat16
i32 = jnp.int32
LOG2E = 1.4426950408889634
LN2 = 0.6931471805599453
MASKED = -1e5
NT = (((1,), (1,)), ((), ()))
NN = (((1,), (0,)), ((), ()))
TN = (((0,), (0,)), ((), ()))
MESH = pl.DeviceIdType.MESH
B = 192
E = 512
V = 4 * B
H = B // 2
XU = [(0, 0), (0, 1), (3, 0), (1, 0), (3, 1), (1, 1), (2, 0), (2, 1)]
PU = [(2, 0), (2, 1), (3, 1), (1, 1), (0, 0), (0, 1), (3, 0), (1, 0)]
N_SEM = 7 * 3 + 8 * 2 + 7 * 3 + 8 + 2 * 7 * 2 + 10


def xs(ry, rx, rc=0):
    return 2 * XU.index((ry, rx)) + rc


def ps(rz, rx):
    return PU.index((rz, rx))


def part(slot, h):
    return pl.ds(slot * B + h * H, H)


def rows(slot):
    return pl.ds(slot * B, B)


def pair_terms(s, row_region, row_match, col_region, col_index, gain, gain2, shift2):
    t = s * gain2 + shift2
    positive = row_match == col_index
    t = jnp.where(positive, -t, jnp.where(row_region != col_region, t, MASKED))
    soft = jnp.log2(1.0 + jnp.exp2(t))
    slope = jnp.exp2(t - soft) * jnp.where(positive, -gain, gain)
    return slope.astype(bf16), soft


def fold(x):
    return jnp.sum(x.reshape(x.shape[0] // 8, 8, 128), axis=0)


def normalize(ref):
    full = ref[...].astype(f32)
    scale = lax.rsqrt(jnp.mean(full * full, axis=-1, keepdims=True) + 1e-06)
    return full * scale, scale


def kernel(
    gain_ref, shift_ref, *hbm_and_rest,
):
    hbm, rest = hbm_and_rest[:4], hbm_and_rest[4:]
    pair_kernel(gain_ref, shift_ref, hbm, *rest)


def pair_kernel(
    gain_ref, shift_ref, hbm,
    loss_ref, sx_ref, sp_ref,
    x_ref, p_ref, region_ref, match_ref, in_sem,
    xb, pb, lab_ref, lx, lp, rr, rm, cr, cj, dx, dp, rc, ry, rz, acc, lsend, lrecv, send_sem, recv_sem,
):
    r, c = lax.axis_index("row"), lax.axis_index("col")
    xl, z = r // 4, r % 4
    y, xh, core = c // 4, (c // 2) % 2, c % 2
    low = c % 4
    cp = (r, c + 1 - 2 * core)
    dxp = ((1 - xl) * 4 + z, c)
    pxp = ((1 - xl) * 4 + z, y * 4 + (1 - xh) * 2 + core)
    xo = (r, y * 4 + (1 - xh) * 2 + core)
    yu, yo, yd = ((r, ((y + k) % 4) * 4 + low) for k in (1, 2, 3))
    zu, zo, zd = ((xl * 4 + (z + k) % 4, c) for k in (1, 2, 3))

    count = [0]
    pending = []

    def send(src, dst, device):
        k = count[0]
        count[0] += 1
        copy = pltpu.make_async_remote_copy(
            src_ref=src, dst_ref=dst, send_sem=send_sem.at[k], recv_sem=recv_sem.at[k],
            device_id=device, device_id_type=MESH,
        )
        copy.start()
        pending.append(copy)
        return copy

    loads = [
        pltpu.make_async_copy(src, dst, in_sem.at[k])
        for k, (src, dst) in enumerate(zip(hbm, (x_ref, p_ref, region_ref, match_ref)))
    ]
    for load in loads:
        load.start()
    barrier = pltpu.get_barrier_semaphore()
    for peer in (cp, dxp, pxp, xo, yu, yo, yd, zu, zo, zd):
        pl.semaphore_signal(barrier, inc=1, device_id=peer, device_id_type=MESH)
    own_x, own_p = xs(0, 0), ps(0, 0)
    acc[...] = jnp.zeros_like(acc)
    for load in loads:
        load.wait()
    xb[rows(own_x), :] = normalize(x_ref)[0].astype(bf16)
    pb[rows(own_p), :] = normalize(p_ref)[0].astype(bf16)
    packed = match_ref[...] * 64 + region_ref[...]
    wide = jnp.concatenate([packed, jnp.zeros((1, 64), i32)], axis=1)
    lab_ref[0] = jnp.concatenate([wide, pltpu.roll(wide, 64, 1)], axis=1)
    lx[own_x] = wide
    lp[own_p] = lab_ref[0]
    pl.semaphore_wait(barrier, 10)

    got = {}

    def send_x(src, dst, device, h):
        if h == 0:
            label = lab_ref.at[0, :, pl.ds(0, 256)] if src == own_x else lx.at[src]
            got["x", dst, "label"] = send(label, lx.at[dst], device)
        got["x", dst, h] = send(xb.at[part(src, h)], xb.at[part(dst, h)], device)

    def send_p(src, dst, device, h):
        if h == 0:
            label = lab_ref.at[0] if src == own_p else lp.at[src]
            got["p", dst, "label"] = send(label, lp.at[dst], device)
        got["p", dst, h] = send(pb.at[part(src, h)], pb.at[part(dst, h)], device)

    def wait(kind, slot, h):
        if h == 0:
            got[kind, slot, "label"].wait_recv()
        got[kind, slot, h].wait_recv()

    def send_core(u):
        src, dst = xs(*u), xs(*u, 1)
        label = lab_ref.at[0, :, pl.ds(0, 256)] if src == own_x else lx.at[src]
        got["core", u] = (send(label, lx.at[dst], cp), send(xb.at[rows(src)], xb.at[rows(dst)], cp))

    def row_info(slot):
        t = jnp.transpose(jnp.broadcast_to(lx[slot], (128, 256)))[0:B]
        rr[rows(slot), :] = t & 63
        rm[rows(slot), :] = t >> 6

    def rows_ready(u):
        row_info(xs(*u))
        for copy in got["core", u]:
            copy.wait_recv()
        row_info(xs(*u, 1))

    def base(rz_, rx):
        zz = (z + rz_) % 4
        if rx == 0:
            return ((xl * 4 + zz) * 16 + y * 4 + xh * 2 + core) * B
        return (((1 - xl) * 4 + zz) * 16 + y * 4 + (1 - xh) * 2 + core) * B

    def col_info(k0):
        first, second = lp[k0], lp[k0 + 1]
        base0, base1 = base(*PU[k0]), base(*PU[k0 + 1])
        lane = lax.broadcasted_iota(i32, (1, 128), 1)
        parts = (first[:, 0:128], first[:, 128:256] + second[:, 256:384], second[:, 384:512])
        for k in range(3):
            at = lane + k * 128
            cs = pl.ds(k0 * B + k * 128, 128)
            cr[:, cs] = parts[k] & 63
            cj[:, cs] = jnp.where(at < B, base0 + at, base1 + at - B)

    for h in (0, 1):
        send_x(own_x, xs(0, 1), dxp, h)
        send_p(own_p, ps(0, 1), pxp, h)
        send_x(own_x, xs(3, 0), yu, h)
        send_x(own_x, xs(1, 0), yd, h)
        send_p(own_p, ps(3, 0), zu, h)
        send_p(own_p, ps(1, 0), zd, h)
    send_core((0, 0))

    gain = gain_ref[...] / E
    gain2 = gain * LOG2E
    shift2 = shift_ref[...] * LOG2E

    def tile(v, c0, width, new_row=False, new_col=False, add_col=None):
        r0 = v * V
        x = xb[pl.ds(r0, V), :]
        p = pb[pl.ds(c0, width), :]
        s = lax.dot_general(x, p, NT, preferred_element_type=f32)
        region, match = rr[pl.ds(r0, V), :], rm[pl.ds(r0, V), :]
        slopes, total = [], None
        for k in range(width // 128):
            cs = pl.ds(c0 + k * 128, 128)
            slope, soft = pair_terms(
                s[:, k * 128 : (k + 1) * 128], region, match, cr[:, cs], cj[:, cs], gain, gain2, shift2
            )
            slopes.append(slope)
            soft = fold(soft)
            total = soft if total is None else total + soft
        acc[...] += total
        g = jnp.concatenate(slopes, axis=1)
        d_row = lax.dot_general(g, p, NN, preferred_element_type=f32)
        dx[pl.ds(r0, V), :] = d_row if new_row else dx[pl.ds(r0, V), :] + d_row
        cut = width if new_col else 0 if add_col is None else add_col - c0
        for lo, hi, new in ((0, cut, True), (cut, width, False)):
            if lo < hi:
                d_col = lax.dot_general(g[:, lo:hi], x, TN, preferred_element_type=f32)
                at = pl.ds(c0 + lo, hi - lo)
                dp[at, :] = d_col if new else dp[at, :] + d_col

    C1, END = 512, 2 * V

    def cols(v, lo, hi, **new):
        tile(v, lo, hi - lo, **new)

    for h in (0, 1):
        wait("x", xs(3, 0), h)
        send_x(xs(3, 0), xs(2, 0), yu, h)
        wait("p", ps(3, 0), h)
        send_p(ps(3, 0), ps(2, 0), zu, h)
        wait("x", xs(0, 1), h)
        send_x(xs(0, 1), xs(1, 1), yd, h)
        wait("p", ps(0, 1), h)
        send_p(ps(0, 1), ps(1, 1), zd, h)
    for h in (0, 1):
        send_x(xs(0, 1), xs(3, 1), yu, h)
        send_p(ps(0, 1), ps(3, 1), zu, h)
    send_core((0, 1))
    send_core((3, 0))
    for h in (0, 1):
        wait("x", xs(1, 0), h)
    send_core((1, 0))
    for h in (0, 1):
        wait("p", ps(1, 0), h)
    col_info(4)
    col_info(6)
    rows_ready((0, 0))
    rows_ready((0, 1))
    cols(0, V, V + 384, new_row=True, new_col=True)
    for h in (0, 1):
        wait("x", xs(1, 1), h)
        send_x(xs(1, 1), xs(2, 1), yd, h)
        wait("p", ps(1, 1), h)
        send_p(ps(1, 1), ps(2, 1), zd, h)
        if h == 0:
            cols(0, V + 384, END, new_col=True)
    send_core((1, 1))
    for h in (0, 1):
        wait("x", xs(2, 0), h)
    send_core((2, 0))
    rows_ready((3, 0))
    rows_ready((1, 0))
    cols(1, V, END, new_row=True)
    rows_ready((2, 0))

    for h in (0, 1):
        wait("x", xs(2, 1), h)
    send_core((2, 1))
    for h in (0, 1):
        wait("x", xs(3, 1), h)
    send_core((3, 1))
    for u in ((2, 0), (2, 1), (3, 1)):
        for h in (0, 1):
            wait("p", ps(*u), h)
    col_info(0)
    col_info(2)
    rows_ready((2, 1))
    cols(3, 0, END, new_row=True, add_col=V)

    half = {}
    back = {}

    def to_core(u):
        half[u] = send(dx.at[rows(xs(*u, 1))], rc.at[XU.index(u)], cp)

    def add_core(u):
        half[u].wait_recv()
        dx[rows(xs(*u)), :] += rc[XU.index(u)]

    def send_dx(u, k, device, h):
        back["x", k, h] = send(dx.at[part(xs(*u), h)], ry.at[k, pl.ds(h * H, H)], device)

    def send_dp(u, k, device, h):
        back["p", k, h] = send(dp.at[part(ps(*u), h)], rz.at[k, pl.ds(h * H, H)], device)

    def add_dx(u, k, h):
        back["x", k, h].wait_recv()
        dx[part(xs(*u), h), :] += ry[k, pl.ds(h * H, H)]

    def add_dp(u, k, h):
        back["p", k, h].wait_recv()
        dp[part(ps(*u), h), :] += rz[k, pl.ds(h * H, H)]

    ring = {}

    def loss_send(k, peers):
        for n, peer in enumerate(peers):
            ring[k, n] = send(lsend.at[k], lrecv.at[3 * k + n], peer)

    def loss_add(k, n):
        for m in range(n):
            ring[k, m].wait_recv()
        if n == 1:
            lsend[k + 1] = lsend[k] + lrecv[3 * k]
        else:
            lsend[k + 1] = (lsend[k] + lrecv[3 * k]) + (lrecv[3 * k + 1] + lrecv[3 * k + 2])

    to_core((2, 0))
    to_core((2, 1))
    cols(0, 0, C1)
    add_core((2, 0))
    add_core((2, 1))
    for h in (0, 1):
        send_dx((2, 0), 0, yd, h)
        send_dx((2, 1), 1, yu, h)
    cols(1, 0, C1)
    rows_ready((3, 1))
    rows_ready((1, 1))
    cols(2, 0, C1, new_row=True)
    for h in (0, 1):
        send_dp((2, 0), 0, zd, h)
        send_dp((2, 1), 1, zu, h)
    cols(2, C1, END)
    to_core((1, 1))
    to_core((3, 1))
    send_dp((0, 1), 6, pxp, 1)
    cols(0, C1, V)
    add_core((1, 1))
    add_core((3, 1))
    send_dx((3, 1), 3, dxp, 1)
    send_dx((3, 1), 3, yd, 0)
    add_dx((1, 1), 1, 0)
    send_dx((1, 1), 5, yu, 0)
    cols(1, C1, V)
    lsend[0] = jnp.sum(acc[...], axis=0, keepdims=True)
    loss_send(0, (cp,))
    for u in ((3, 0), (1, 0), (0, 1), (0, 0)):
        to_core(u)
    send_dp((3, 1), 3, pxp, 1)
    send_dp((3, 1), 3, zd, 0)
    add_dx((1, 1), 1, 1)
    send_dx((1, 1), 5, dxp, 1)
    add_dp((1, 1), 1, 0)
    send_dp((1, 1), 5, zu, 0)
    add_dp((3, 0), 0, 0)
    send_dp((3, 0), 2, zd, 0)
    send_dp((1, 0), 4, zu, 0)
    loss_add(0, 1)
    loss_send(1, (yo, yu, yd))
    add_core((3, 0))
    add_dx((3, 0), 0, 0)
    send_dx((3, 0), 2, yd, 0)
    add_core((1, 0))
    send_dx((1, 0), 4, yu, 0)
    add_core((0, 1))
    add_core((0, 0))
    add_dx((3, 0), 0, 1)
    add_dp((1, 1), 1, 1)
    send_dp((1, 1), 5, pxp, 1)
    add_dp((3, 0), 0, 1)
    add_dx((0, 1), 3, 0)
    add_dx((0, 1), 5, 0)
    send_dx((0, 1), 6, dxp, 0)
    add_dx((3, 0), 3, 1)
    send_dx((3, 0), 2, yd, 1)
    loss_add(1, 3)
    loss_send(2, (xo, dxp, pxp))
    send_dx((0, 1), 6, dxp, 1)
    add_dp((3, 0), 3, 1)
    send_dp((3, 0), 2, zd, 1)
    add_dx((1, 0), 5, 1)
    send_dx((1, 0), 4, yu, 1)
    add_dp((0, 1), 3, 0)
    add_dp((0, 1), 5, 0)
    send_dp((0, 1), 6, pxp, 0)
    add_dp((1, 0), 5, 1)
    loss_add(2, 3)
    loss_send(3, (zo, zu, zd))
    send_dp((1, 0), 4, zu, 1)
    add_dx((0, 0), 2, 0)
    add_dx((0, 0), 4, 0)
    add_dp((0, 0), 6, 1)
    add_dx((0, 0), 6, 0)
    add_dp((0, 0), 2, 0)
    add_dp((0, 0), 4, 0)
    add_dx((0, 0), 4, 1)
    add_dx((0, 0), 2, 1)
    add_dx((0, 0), 6, 1)
    sx_ref[...] = dx[rows(own_x), :]
    loss_add(3, 3)
    loss_ref[...] = lsend[4]
    add_dp((0, 0), 2, 1)
    add_dp((0, 0), 6, 0)
    add_dp((0, 0), 4, 1)
    sp_ref[...] = dp[rows(own_p), :]
    for copy in pending:
        copy.wait_send()
    assert count[0] == N_SEM


def finish(x_ref, p_ref, sx_ref, sp_ref, sum_ref, loss_ref, gx_ref, gp_ref):
    for ref, sums, out in ((x_ref, sx_ref, gx_ref), (p_ref, sp_ref, gp_ref)):
        full, scale = normalize(ref)
        dnorm = sums[...]
        out[...] = scale * (dnorm - full * jnp.mean(dnorm * full, axis=-1, keepdims=True))
    n = float(128 * B)
    loss_ref[0] = jnp.sum(sum_ref[...]) * LN2 / (n * n)


def on_device(lensed, theta, region, match, gain, shift):
    vmem = pl.BlockSpec(memory_space=pltpu.VMEM)
    smem = pl.BlockSpec(memory_space=pltpu.SMEM)
    block = jax.ShapeDtypeStruct((B, E), f32)
    total, sum_x, sum_p = pl.pallas_call(
        kernel,
        out_shape=(jax.ShapeDtypeStruct((1, 128), f32), block, block),
        in_specs=[vmem] * 2 + [pl.BlockSpec(memory_space=pltpu.HBM)] * 4,
        out_specs=(vmem,) * 3,
        scratch_shapes=[
            pltpu.VMEM((B, E), bf16),
            pltpu.VMEM((B, E), bf16),
            pltpu.VMEM((1, B), i32),
            pltpu.VMEM((1, B), i32),
            pltpu.SemaphoreType.DMA((4,)),
            pltpu.VMEM((16 * B, E), bf16),
            pltpu.VMEM((8 * B, E), bf16),
            pltpu.VMEM((1, 1, 512), i32),
            pltpu.VMEM((16, 1, 256), i32),
            pltpu.VMEM((8, 1, 512), i32),
            pltpu.VMEM((16 * B, 128), i32),
            pltpu.VMEM((16 * B, 128), i32),
            pltpu.VMEM((1, 8 * B), i32),
            pltpu.VMEM((1, 8 * B), i32),
            pltpu.VMEM((16 * B, E), f32),
            pltpu.VMEM((8 * B, E), f32),
            pltpu.VMEM((8, B, E), f32),
            pltpu.VMEM((7, B, E), f32),
            pltpu.VMEM((7, B, E), f32),
            pltpu.VMEM((8, 128), f32),
            pltpu.VMEM((5, 1, 128), f32),
            pltpu.VMEM((12, 1, 128), f32),
            pltpu.SemaphoreType.DMA((N_SEM,)),
            pltpu.SemaphoreType.DMA((N_SEM,)),
        ],
        compiler_params=pltpu.CompilerParams(
            collective_id=0, has_side_effects=True, vmem_limit_bytes=67043328
        ),
        name="pairs",
    )(gain.reshape(1, 1), shift.reshape(1, 1), lensed, theta, region.reshape(1, B), match.reshape(1, B))
    return pl.pallas_call(
        finish,
        out_shape=(jax.ShapeDtypeStruct((1,), f32), block, block),
        in_specs=[vmem] * 5,
        out_specs=(smem, vmem, vmem),
        compiler_params=pltpu.CompilerParams(vmem_limit_bytes=67043328),
        name="finish",
    )(lensed, theta, sum_x, sum_p, total)


def solution(mesh):
    both = ("row", "col")
    in_specs = (P(both, None), P(both, None), P(both), P(both), P(), P())
    out_specs = (P(), P(both, None), P(both, None))
    return jax.shard_map(
        on_device, mesh=mesh, in_specs=in_specs, out_specs=out_specs, check_vma=False
    )
```

time: 84.3 us -> 70.6 us (0.84)
  Pallas kernels: 76.8 us -> 68.3 us
  local copies, waits for them, and re-layouts: 2.58 us -> 0 us
  between operations: 3.77 us -> 2.09 us
    pallas_call x1 -> x2, Pallas kernels: 76.8 us -> 68.3 us  [the longest x1 65.9 us: on_device(): pl.pallas_call(kernel, out_shape=(jax.ShapeDtypeStruct((1, 128), f32), bl...]
    unnamed x8 -> x0, local copies, waits for them, and re-layouts: 2.58 us -> none
where the time goes in v3:
time: 70.6 us; the launch traced here: 70.4 us
  Pallas kernels  68.3 us (97%)
  between operations  2.09 us (3%)
    pallas_call x1, Pallas kernels, on_device(): pl.pallas_call(kernel, out_shape=(jax.ShapeDtypeStruct((1, 128), f32), bl...  65.9 us
    pallas_call x1, Pallas kernels, on_device(): pl.pallas_call(finish, out_shape=(jax.ShapeDtypeStruct((1,), f32), block,...  2.4 us

profile of v3, /device:TPU:0, one launch (start us, length us, event | category | flops | bytes accessed | tf_op | source)
XLA Modules:
  0.0 70.4 jit_solution(16155678030560580970)
XLA Ops:
  1.9 65.9 %pairs.1 = (f32[1,128]{1,0:T(1,128)}, f32[192,512]{1,0:T(8,128)}, f32[192,512]{1,0:T(8,128)}) custom-call(f32[1,1]{1,0:T(1,128)} %bitcast.4.gain_ref, f32[1,1]{1,0:T(1,128)} %bitcast.5.shift_ref, bf16[192,512]{1,0:T(8,128)(2,1)} %x_ref.1, bf16[192,512]{1,0:T(8,128)(2,1)} %p_ref.1, s32[1,192]{1,0:T(1,128)} %bitcast.6, s32[1,192]{1,0:T(1,128)} %bitcast.7), custom_call_target="tpu_custom_call" | custom-call | tf_op jit(solution)/shard_map/pairs/pallas_call | solution.py:416
  67.8 2.4 %finish.1 = (f32[1]{0:T(128)}, f32[192,512]{1,0:T(8,128)}, f32[192,512]{1,0:T(8,128)}) custom-call(bf16[192,512]{1,0:T(8,128)(2,1)} %x_ref.1, bf16[192,512]{1,0:T(8,128)(2,1)} %p_ref.1, f32[192,512]{1,0:T(8,128)} %get-tuple-element.6.sx_ref, f32[192,512]{1,0:T(8,128)} %get-tuple-element.7.sp_ref, f32[1,128]{1,0:T(1,128)} %get-tuple-element.8.sum_ref), custom_call_target="tpu_custom_call" | custom-call | tf_op jit(solution)/shard_map/finish/pallas_call | solution.py:452

commit v4 on v3

--- a/solution.py
+++ b/solution.py
@@ -68,7 +68,7 @@
 
 def pair_kernel(
     gain_ref, shift_ref, hbm,
-    loss_ref, sx_ref, sp_ref,
+    loss_ref, sx_ref, sp_ref, xo_ref, po_ref,
     x_ref, p_ref, region_ref, match_ref, in_sem,
     xb, pb, lab_ref, lx, lp, rr, rm, cr, cj, dx, dp, rc, ry, rz, acc, lsend, lrecv, send_sem, recv_sem,
 ):
@@ -112,6 +112,8 @@
         load.wait()
     xb[rows(own_x), :] = normalize(x_ref)[0].astype(bf16)
     pb[rows(own_p), :] = normalize(p_ref)[0].astype(bf16)
+    xo_ref[...] = x_ref[...]
+    po_ref[...] = p_ref[...]
     packed = match_ref[...] * 64 + region_ref[...]
     wide = jnp.concatenate([packed, jnp.zeros((1, 64), i32)], axis=1)
     lab_ref[0] = jnp.concatenate([wide, pltpu.roll(wide, 64, 1)], axis=1)
@@ -319,7 +321,7 @@
     rows_ready((3, 1))
     rows_ready((1, 1))
     cols(2, 0, C1, new_row=True)
-    for h in (0, 1):
+    for h in (1, 0):
         send_dp((2, 0), 0, zd, h)
         send_dp((2, 1), 1, zu, h)
     cols(2, C1, END)
@@ -338,50 +340,52 @@
     loss_send(0, (cp,))
     for u in ((3, 0), (1, 0), (0, 1), (0, 0)):
         to_core(u)
-    send_dp((3, 1), 3, pxp, 1)
-    send_dp((3, 1), 3, zd, 0)
     add_dx((1, 1), 1, 1)
     send_dx((1, 1), 5, dxp, 1)
+    add_dp((1, 1), 1, 1)
+    send_dp((1, 1), 5, pxp, 1)
+    send_dp((3, 1), 3, pxp, 1)
+    loss_add(0, 1)
+    loss_send(1, (zo, zu, zd))
+    send_dp((3, 1), 3, zd, 0)
+    send_dp((1, 0), 4, zu, 0)
+    add_core((3, 0))
+    add_dx((3, 0), 0, 0)
+    add_core((1, 0))
+    add_core((0, 1))
+    add_core((0, 0))
+    add_dx((3, 0), 0, 1)
+    add_dp((3, 0), 0, 1)
     add_dp((1, 1), 1, 0)
     send_dp((1, 1), 5, zu, 0)
     add_dp((3, 0), 0, 0)
     send_dp((3, 0), 2, zd, 0)
-    send_dp((1, 0), 4, zu, 0)
-    loss_add(0, 1)
-    loss_send(1, (yo, yu, yd))
-    add_core((3, 0))
-    add_dx((3, 0), 0, 0)
+    loss_add(1, 3)
+    loss_send(2, (yo, yu, yd))
     send_dx((3, 0), 2, yd, 0)
-    add_core((1, 0))
     send_dx((1, 0), 4, yu, 0)
-    add_core((0, 1))
-    add_core((0, 0))
-    add_dx((3, 0), 0, 1)
-    add_dp((1, 1), 1, 1)
-    send_dp((1, 1), 5, pxp, 1)
-    add_dp((3, 0), 0, 1)
     add_dx((0, 1), 3, 0)
     add_dx((0, 1), 5, 0)
+    loss_add(2, 3)
+    loss_send(3, (xo, dxp, pxp))
     send_dx((0, 1), 6, dxp, 0)
+    send_dx((0, 1), 6, dxp, 1)
     add_dx((3, 0), 3, 1)
     send_dx((3, 0), 2, yd, 1)
-    loss_add(1, 3)
-    loss_send(2, (xo, dxp, pxp))
-    send_dx((0, 1), 6, dxp, 1)
+    add_dx((1, 0), 5, 1)
+    send_dx((1, 0), 4, yu, 1)
+    add_dp((1, 0), 5, 1)
+    send_dp((1, 0), 4, zu, 1)
     add_dp((3, 0), 3, 1)
     send_dp((3, 0), 2, zd, 1)
-    add_dx((1, 0), 5, 1)
-    send_dx((1, 0), 4, yu, 1)
     add_dp((0, 1), 3, 0)
     add_dp((0, 1), 5, 0)
     send_dp((0, 1), 6, pxp, 0)
-    add_dp((1, 0), 5, 1)
-    loss_add(2, 3)
-    loss_send(3, (zo, zu, zd))
-    send_dp((1, 0), 4, zu, 1)
     add_dx((0, 0), 2, 0)
     add_dx((0, 0), 4, 0)
     add_dp((0, 0), 6, 1)
+    loss_add(3, 3)
+    loss_ref[...] = lsend[4]
     add_dx((0, 0), 6, 0)
     add_dp((0, 0), 2, 0)
     add_dp((0, 0), 4, 0)
@@ -389,11 +393,9 @@
     add_dx((0, 0), 2, 1)
     add_dx((0, 0), 6, 1)
     sx_ref[...] = dx[rows(own_x), :]
-    loss_add(3, 3)
-    loss_ref[...] = lsend[4]
+    add_dp((0, 0), 4, 1)
     add_dp((0, 0), 2, 1)
     add_dp((0, 0), 6, 0)
-    add_dp((0, 0), 4, 1)
     sp_ref[...] = dp[rows(own_p), :]
     for copy in pending:
         copy.wait_send()
@@ -411,13 +413,17 @@
 
 def on_device(lensed, theta, region, match, gain, shift):
     vmem = pl.BlockSpec(memory_space=pltpu.VMEM)
+    lensed, theta, region, match = (
+        pltpu.with_memory_space_constraint(a, pltpu.HBM) for a in (lensed, theta, region.reshape(1, B), match.reshape(1, B))
+    )
     smem = pl.BlockSpec(memory_space=pltpu.SMEM)
     block = jax.ShapeDtypeStruct((B, E), f32)
-    total, sum_x, sum_p = pl.pallas_call(
+    half = jax.ShapeDtypeStruct((B, E), bf16)
+    total, sum_x, sum_p, x, p = pl.pallas_call(
         kernel,
-        out_shape=(jax.ShapeDtypeStruct((1, 128), f32), block, block),
+        out_shape=(jax.ShapeDtypeStruct((1, 128), f32), block, block, half, half),
         in_specs=[vmem] * 2 + [pl.BlockSpec(memory_space=pltpu.HBM)] * 4,
-        out_specs=(vmem,) * 3,
+        out_specs=(vmem,) * 5,
         scratch_shapes=[
             pltpu.VMEM((B, E), bf16),
             pltpu.VMEM((B, E), bf16),
@@ -445,18 +451,18 @@
             pltpu.SemaphoreType.DMA((N_SEM,)),
         ],
         compiler_params=pltpu.CompilerParams(
-            collective_id=0, has_side_effects=True, vmem_limit_bytes=67043328
+            collective_id=0, has_side_effects=True, vmem_limit_bytes=48 << 20
         ),
         name="pairs",
-    )(gain.reshape(1, 1), shift.reshape(1, 1), lensed, theta, region.reshape(1, B), match.reshape(1, B))
+    )(gain.reshape(1, 1), shift.reshape(1, 1), lensed, theta, region, match)
     return pl.pallas_call(
         finish,
         out_shape=(jax.ShapeDtypeStruct((1,), f32), block, block),
         in_specs=[vmem] * 5,
         out_specs=(smem, vmem, vmem),
-        compiler_params=pltpu.CompilerParams(vmem_limit_bytes=67043328),
+        compiler_params=pltpu.CompilerParams(vmem_limit_bytes=8 << 20),
         name="finish",
-    )(lensed, theta, sum_x, sum_p, total)
+    )(x, p, sum_x, sum_p, total)
 
 
 def solution(mesh):

time: 70.6 us -> 67.8 us (0.960)
  Pallas kernels: 68.3 us -> 65.4 us
    pallas_call x1, Pallas kernels: 65.9 us -> 64.3 us  [on_device(): pl.pallas_call(kernel, out_shape=(jax.ShapeDtypeStruct((1, 128), f32), bl...]
    pallas_call x1, Pallas kernels: 2.4 us -> 1.14 us  [on_device(): pl.pallas_call(finish, out_shape=(jax.ShapeDtypeStruct((1,), f32), block,...]
where the time goes in v4:
time: 67.8 us; the launch traced here: 67.5 us
  Pallas kernels  65.4 us (96%)
  between operations  2.09 us (3%)
    pallas_call x1, Pallas kernels, on_device(): pl.pallas_call(kernel, out_shape=(jax.ShapeDtypeStruct((1, 128), f32), bl...  64.3 us

profile of v4, /device:TPU:0, one launch (start us, length us, event | category | flops | bytes accessed | tf_op | source)
XLA Modules:
  0.0 67.5 jit_solution(5990116327427113915)
XLA Ops:
  1.9 64.3 %pairs.1 = (f32[1,128]{1,0:T(1,128)S(1)}, f32[192,512]{1,0:T(8,128)S(1)}, f32[192,512]{1,0:T(8,128)S(1)}, bf16[192,512]{1,0:T(8,128)(2,1)S(1)}, bf16[192,512]{1,0:T(8,128)(2,1)S(1)}) custom-call(f32[1,1]{1,0:T(1,128)} %bitcast.4.gain_ref, f32[1,1]{1,0:T(1,128)} %bitcast.5.shift_ref, bf16[192,512]{1,0:T(8,128)(2,1)} %hbm_and_rest_0_.1, ...), custom_call_target="tpu_custom_call" | custom-call | tf_op jit(solution)/shard_map/pairs/pallas_call | solution.py:422
  66.2 1.1 %finish.1 = (f32[1]{0:T(128)}, f32[192,512]{1,0:T(8,128)}, f32[192,512]{1,0:T(8,128)}) custom-call(bf16[192,512]{1,0:T(8,128)(2,1)S(1)} %get-tuple-element.8.x_ref, bf16[192,512]{1,0:T(8,128)(2,1)S(1)} %get-tuple-element.9.p_ref, f32[192,512]{1,0:T(8,128)S(1)} %get-tuple-element.10.sx_ref, f32[192,512]{1,0:T(8,128)S(1)} %get-tuple-element.11.sp_ref, ...), custom_call_target="tpu_custom_call" | custom-call | tf_op jit(solution)/shard_map/finish/pallas_call | solution.py:458

commit v5 on v4

--- a/solution.py
+++ b/solution.py
@@ -321,7 +321,7 @@
     rows_ready((3, 1))
     rows_ready((1, 1))
     cols(2, 0, C1, new_row=True)
-    for h in (1, 0):
+    for h in (0, 1):
         send_dp((2, 0), 0, zd, h)
         send_dp((2, 1), 1, zu, h)
     cols(2, C1, END)
@@ -342,12 +342,14 @@
         to_core(u)
     add_dx((1, 1), 1, 1)
     send_dx((1, 1), 5, dxp, 1)
-    add_dp((1, 1), 1, 1)
-    send_dp((1, 1), 5, pxp, 1)
     send_dp((3, 1), 3, pxp, 1)
     loss_add(0, 1)
     loss_send(1, (zo, zu, zd))
     send_dp((3, 1), 3, zd, 0)
+    add_dp((1, 1), 1, 0)
+    send_dp((1, 1), 5, zu, 0)
+    add_dp((3, 0), 0, 0)
+    send_dp((3, 0), 2, zd, 0)
     send_dp((1, 0), 4, zu, 0)
     add_core((3, 0))
     add_dx((3, 0), 0, 0)
@@ -355,32 +357,30 @@
     add_core((0, 1))
     add_core((0, 0))
     add_dx((3, 0), 0, 1)
+    add_dp((1, 1), 1, 1)
+    send_dp((1, 1), 5, pxp, 1)
     add_dp((3, 0), 0, 1)
-    add_dp((1, 1), 1, 0)
-    send_dp((1, 1), 5, zu, 0)
-    add_dp((3, 0), 0, 0)
-    send_dp((3, 0), 2, zd, 0)
     loss_add(1, 3)
     loss_send(2, (yo, yu, yd))
     send_dx((3, 0), 2, yd, 0)
     send_dx((1, 0), 4, yu, 0)
     add_dx((0, 1), 3, 0)
     add_dx((0, 1), 5, 0)
+    send_dx((0, 1), 6, dxp, 0)
+    add_dx((3, 0), 3, 1)
+    send_dx((3, 0), 2, yd, 1)
+    add_dp((3, 0), 3, 1)
+    send_dp((3, 0), 2, zd, 1)
     loss_add(2, 3)
     loss_send(3, (xo, dxp, pxp))
-    send_dx((0, 1), 6, dxp, 0)
     send_dx((0, 1), 6, dxp, 1)
-    add_dx((3, 0), 3, 1)
-    send_dx((3, 0), 2, yd, 1)
     add_dx((1, 0), 5, 1)
     send_dx((1, 0), 4, yu, 1)
-    add_dp((1, 0), 5, 1)
-    send_dp((1, 0), 4, zu, 1)
-    add_dp((3, 0), 3, 1)
-    send_dp((3, 0), 2, zd, 1)
     add_dp((0, 1), 3, 0)
     add_dp((0, 1), 5, 0)
     send_dp((0, 1), 6, pxp, 0)
+    add_dp((1, 0), 5, 1)
+    send_dp((1, 0), 4, zu, 1)
     add_dx((0, 0), 2, 0)
     add_dx((0, 0), 4, 0)
     add_dp((0, 0), 6, 1)

time: 67.8 us -> 67 us (0.988)
  no operation moved by 1% of the time
where the time goes in v5:
time: 67 us; the launch traced here: 66.9 us
  Pallas kernels  64.8 us (97%)
  between operations  2.09 us (3%)
    pallas_call x1, Pallas kernels, on_device(): pl.pallas_call(kernel, out_shape=(jax.ShapeDtypeStruct((1, 128), f32), bl...  63.6 us

profile of v5, /device:TPU:0, one launch (start us, length us, event | category | flops | bytes accessed | tf_op | source)
XLA Modules:
  0.0 66.9 jit_solution(17671627099815372485)
XLA Ops:
  1.9 63.6 %pairs.1 = (f32[1,128]{1,0:T(1,128)S(1)}, f32[192,512]{1,0:T(8,128)S(1)}, f32[192,512]{1,0:T(8,128)S(1)}, bf16[192,512]{1,0:T(8,128)(2,1)S(1)}, bf16[192,512]{1,0:T(8,128)(2,1)S(1)}) custom-call(f32[1,1]{1,0:T(1,128)} %bitcast.4.gain_ref, f32[1,1]{1,0:T(1,128)} %bitcast.5.shift_ref, bf16[192,512]{1,0:T(8,128)(2,1)} %hbm_and_rest_0_.1, ...), custom_call_target="tpu_custom_call" | custom-call | tf_op jit(solution)/shard_map/pairs/pallas_call | solution.py:422
  65.6 1.1 %finish.1 = (f32[1]{0:T(128)}, f32[192,512]{1,0:T(8,128)}, f32[192,512]{1,0:T(8,128)}) custom-call(bf16[192,512]{1,0:T(8,128)(2,1)S(1)} %get-tuple-element.8.x_ref, bf16[192,512]{1,0:T(8,128)(2,1)S(1)} %get-tuple-element.9.p_ref, f32[192,512]{1,0:T(8,128)S(1)} %get-tuple-element.10.sx_ref, f32[192,512]{1,0:T(8,128)S(1)} %get-tuple-element.11.sp_ref, ...), custom_call_target="tpu_custom_call" | custom-call | tf_op jit(solution)/shard_map/finish/pallas_call | solution.py:458

commit v6 on v5

--- a/solution.py
+++ b/solution.py
@@ -19,6 +19,7 @@
 E = 512
 V = 4 * B
 H = B // 2
+CUT_X, CUT_P = 112, 112
 XU = [(0, 0), (0, 1), (3, 0), (1, 0), (3, 1), (1, 1), (2, 0), (2, 1)]
 PU = [(2, 0), (2, 1), (3, 1), (1, 1), (0, 0), (0, 1), (3, 0), (1, 0)]
 N_SEM = 7 * 3 + 8 * 2 + 7 * 3 + 8 + 2 * 7 * 2 + 10
@@ -281,19 +282,22 @@
         half[u].wait_recv()
         dx[rows(xs(*u)), :] += rc[XU.index(u)]
 
+    def cut(slot, h, first):
+        return pl.ds(slot * B + h * first, B - first if h else first)
+
     def send_dx(u, k, device, h):
-        back["x", k, h] = send(dx.at[part(xs(*u), h)], ry.at[k, pl.ds(h * H, H)], device)
+        back["x", k, h] = send(dx.at[cut(xs(*u), h, CUT_X)], ry.at[k, cut(0, h, CUT_X)], device)
 
     def send_dp(u, k, device, h):
-        back["p", k, h] = send(dp.at[part(ps(*u), h)], rz.at[k, pl.ds(h * H, H)], device)
+        back["p", k, h] = send(dp.at[cut(ps(*u), h, CUT_P)], rz.at[k, cut(0, h, CUT_P)], device)
 
     def add_dx(u, k, h):
         back["x", k, h].wait_recv()
-        dx[part(xs(*u), h), :] += ry[k, pl.ds(h * H, H)]
+        dx[cut(xs(*u), h, CUT_X), :] += ry[k, cut(0, h, CUT_X)]
 
     def add_dp(u, k, h):
         back["p", k, h].wait_recv()
-        dp[part(ps(*u), h), :] += rz[k, pl.ds(h * H, H)]
+        dp[cut(ps(*u), h, CUT_P), :] += rz[k, cut(0, h, CUT_P)]
 
     ring = {}
 

time: 67 us -> 66.2 us (0.988)
  Pallas kernels: 64.8 us -> 63.3 us
    pallas_call x1, Pallas kernels: 63.6 us -> 62.2 us  [on_device(): pl.pallas_call(kernel, out_shape=(jax.ShapeDtypeStruct((1, 128), f32), bl...]
where the time goes in v6:
time: 66.2 us; the launch traced here: 65.4 us
  Pallas kernels  63.3 us (96%)
  between operations  2.09 us (3%)
    pallas_call x1, Pallas kernels, on_device(): pl.pallas_call(kernel, out_shape=(jax.ShapeDtypeStruct((1, 128), f32), bl...  62.2 us

profile of v6, /device:TPU:0, one launch (start us, length us, event | category | flops | bytes accessed | tf_op | source)
XLA Modules:
  0.0 65.4 jit_solution(10501342000358800861)
XLA Ops:
  1.9 62.2 %pairs.1 = (f32[1,128]{1,0:T(1,128)S(1)}, f32[192,512]{1,0:T(8,128)S(1)}, f32[192,512]{1,0:T(8,128)S(1)}, bf16[192,512]{1,0:T(8,128)(2,1)S(1)}, bf16[192,512]{1,0:T(8,128)(2,1)S(1)}) custom-call(f32[1,1]{1,0:T(1,128)} %bitcast.4.gain_ref, f32[1,1]{1,0:T(1,128)} %bitcast.5.shift_ref, bf16[192,512]{1,0:T(8,128)(2,1)} %hbm_and_rest_0_.1, ...), custom_call_target="tpu_custom_call" | custom-call | tf_op jit(solution)/shard_map/pairs/pallas_call | solution.py:426
  64.1 1.1 %finish.1 = (f32[1]{0:T(128)}, f32[192,512]{1,0:T(8,128)}, f32[192,512]{1,0:T(8,128)}) custom-call(bf16[192,512]{1,0:T(8,128)(2,1)S(1)} %get-tuple-element.8.x_ref, bf16[192,512]{1,0:T(8,128)(2,1)S(1)} %get-tuple-element.9.p_ref, f32[192,512]{1,0:T(8,128)S(1)} %get-tuple-element.10.sx_ref, f32[192,512]{1,0:T(8,128)S(1)} %get-tuple-element.11.sp_ref, ...), custom_call_target="tpu_custom_call" | custom-call | tf_op jit(solution)/shard_map/finish/pallas_call | solution.py:462

commit v7 on v6

--- a/solution.py
+++ b/solution.py
@@ -257,6 +257,7 @@
     rows_ready((1, 0))
     cols(1, V, END, new_row=True)
     rows_ready((2, 0))
+    rows_ready((1, 1))
 
     for h in (0, 1):
         wait("x", xs(2, 1), h)
@@ -264,6 +265,7 @@
     for h in (0, 1):
         wait("x", xs(3, 1), h)
     send_core((3, 1))
+    row_info(xs(3, 1))
     for u in ((2, 0), (2, 1), (3, 1)):
         for h in (0, 1):
             wait("p", ps(*u), h)
@@ -322,8 +324,9 @@
         send_dx((2, 0), 0, yd, h)
         send_dx((2, 1), 1, yu, h)
     cols(1, 0, C1)
-    rows_ready((3, 1))
-    rows_ready((1, 1))
+    for copy in got["core", (3, 1)]:
+        copy.wait_recv()
+    row_info(xs(3, 1, 1))
     cols(2, 0, C1, new_row=True)
     for h in (0, 1):
         send_dp((2, 0), 0, zd, h)

time: 66.2 us -> 65.9 us (level)
  no operation moved by 1% of the time
where the time goes in v7:
time: 65.9 us; the launch traced here: 65.2 us
  Pallas kernels  63.1 us (96%)
  between operations  2.09 us (3%)
    pallas_call x1, Pallas kernels, on_device(): pl.pallas_call(kernel, out_shape=(jax.ShapeDtypeStruct((1, 128), f32), bl...  62 us

profile of v7, /device:TPU:0, one launch (start us, length us, event | category | flops | bytes accessed | tf_op | source)
XLA Modules:
  0.0 65.2 jit_solution(11435524092203249138)
XLA Ops:
  1.9 62.0 %pairs.1 = (f32[1,128]{1,0:T(1,128)S(1)}, f32[192,512]{1,0:T(8,128)S(1)}, f32[192,512]{1,0:T(8,128)S(1)}, bf16[192,512]{1,0:T(8,128)(2,1)S(1)}, bf16[192,512]{1,0:T(8,128)(2,1)S(1)}) custom-call(f32[1,1]{1,0:T(1,128)} %bitcast.4.gain_ref, f32[1,1]{1,0:T(1,128)} %bitcast.5.shift_ref, bf16[192,512]{1,0:T(8,128)(2,1)} %hbm_and_rest_0_.1, ...), custom_call_target="tpu_custom_call" | custom-call | tf_op jit(solution)/shard_map/pairs/pallas_call | solution.py:429
  63.9 1.1 %finish.1 = (f32[1]{0:T(128)}, f32[192,512]{1,0:T(8,128)}, f32[192,512]{1,0:T(8,128)}) custom-call(bf16[192,512]{1,0:T(8,128)(2,1)S(1)} %get-tuple-element.8.x_ref, bf16[192,512]{1,0:T(8,128)(2,1)S(1)} %get-tuple-element.9.p_ref, f32[192,512]{1,0:T(8,128)S(1)} %get-tuple-element.10.sx_ref, f32[192,512]{1,0:T(8,128)S(1)} %get-tuple-element.11.sp_ref, ...), custom_call_target="tpu_custom_call" | custom-call | tf_op jit(solution)/shard_map/finish/pallas_call | solution.py:465

commit v8 on v7

--- a/solution.py
+++ b/solution.py
@@ -19,7 +19,7 @@
 E = 512
 V = 4 * B
 H = B // 2
-CUT_X, CUT_P = 112, 112
+CUT_X, CUT_P = 120, 112
 XU = [(0, 0), (0, 1), (3, 0), (1, 0), (3, 1), (1, 1), (2, 0), (2, 1)]
 PU = [(2, 0), (2, 1), (3, 1), (1, 1), (0, 0), (0, 1), (3, 0), (1, 0)]
 N_SEM = 7 * 3 + 8 * 2 + 7 * 3 + 8 + 2 * 7 * 2 + 10

time: 65.9 us -> 65.9 us (level)
  no operation moved by 1% of the time
where the time goes in v8:
time: 65.9 us; the launch traced here: 65.2 us
  Pallas kernels  63.1 us (96%)
  between operations  2.09 us (3%)
    pallas_call x1, Pallas kernels, on_device(): pl.pallas_call(kernel, out_shape=(jax.ShapeDtypeStruct((1, 128), f32), bl...  62 us

profile of v8, /device:TPU:0, one launch (start us, length us, event | category | flops | bytes accessed | tf_op | source)
XLA Modules:
  0.0 65.2 jit_solution(5259635985861959607)
XLA Ops:
  1.9 62.0 %pairs.1 = (f32[1,128]{1,0:T(1,128)S(1)}, f32[192,512]{1,0:T(8,128)S(1)}, f32[192,512]{1,0:T(8,128)S(1)}, bf16[192,512]{1,0:T(8,128)(2,1)S(1)}, bf16[192,512]{1,0:T(8,128)(2,1)S(1)}) custom-call(f32[1,1]{1,0:T(1,128)} %bitcast.4.gain_ref, f32[1,1]{1,0:T(1,128)} %bitcast.5.shift_ref, bf16[192,512]{1,0:T(8,128)(2,1)} %hbm_and_rest_0_.1, ...), custom_call_target="tpu_custom_call" | custom-call | tf_op jit(solution)/shard_map/pairs/pallas_call | solution.py:429
  63.9 1.1 %finish.1 = (f32[1]{0:T(128)}, f32[192,512]{1,0:T(8,128)}, f32[192,512]{1,0:T(8,128)}) custom-call(bf16[192,512]{1,0:T(8,128)(2,1)S(1)} %get-tuple-element.8.x_ref, bf16[192,512]{1,0:T(8,128)(2,1)S(1)} %get-tuple-element.9.p_ref, f32[192,512]{1,0:T(8,128)S(1)} %get-tuple-element.10.sx_ref, f32[192,512]{1,0:T(8,128)S(1)} %get-tuple-element.11.sp_ref, ...), custom_call_target="tpu_custom_call" | custom-call | tf_op jit(solution)/shard_map/finish/pallas_call | solution.py:465
